TPU v7x, 256 devices: a whole 4x4x8 slice. The times are simulated.
256 devices in a mesh: tm: 64 (over x_hi, z, y), space: 4 (over x_lo, core).
Axes of the slice: x: 4 (x_hi: 2, x_lo: 2; x = x_hi * 2 + x_lo), y: 4, z: 8, core: 2. Of those that a mesh axis runs over, the one named last changes fastest.
Arguments:
- volume: float32 [64, 16, 256, 256], P('tm', 'space'), may hold values from -6 to 6
- prior_image: float32 [64, 16, 256, 256], P('tm', 'space'), may hold values from -6 to 6
- dual_pairs: float32 [64, 4, 16, 256, 256], P('tm', None, 'space'), may hold values from -0.3 to 0.3
- pair_cycle: int32 [64, 4], P('tm'), may hold values from -2 to 2, as said below
- pair_offset: int32 [64, 4], P('tm'), may hold values from -3 to 3
Outputs:
- volume_next: float32 [64, 16, 256, 256], P('tm', 'space')
- dual_next: float32 [64, 4, 16, 256, 256], P('tm', None, 'space')
Inputs may be any that keep to these rules, and one draw needn't show every extreme that they name: `pair_cycle`: each frame has at least one filled slot; filled slots come first, name distinct cycle offsets, and always name a partner frame inside 0 .. 63.
All inputs are finite; a program needn't handle non-finite values.
Results may differ from a plain program's by a relative error of at most 0.0003.
Values sent between devices are 32-bit elements; how exact they have to be, the bound alone decides.
A program may use at most 64 MiB of HBM per device.

v0:
```python
import functools

import jax
import jax.numpy as jnp
from jax import lax
from jax.experimental import pallas as pl
from jax.experimental.pallas import tpu as pltpu
from jax.sharding import PartitionSpec as P

MESH = pl.DeviceIdType.MESH

NZ, NY = 4, 256
LANES, HALVES = 128, 2
PAD = 8
ROWS = NY + 2 * PAD
CHUNK = 64

NAMES = []
for stem, slices in (
    ("P", (0, 1, 2, 3)),
    ("M", (0, 1, 2, 3)),
    ("PR", (0, 1)),
    ("MR", (2, 3)),
    ("XW", (0, 1, 2, 3)),
    ("XO", (0, 1, 2, 3)),
    ("XV", (0, 1, 2, 3)),
    ("HL", (0, 1, 2, 3, 4)),
    ("HH", (0, 1, 2, 3, 4)),
    ("FX", (0, 1, 2, 3)),
    ("XD", (0, 1, 2, 3)),
    ("FO", (0, 1, 2, 3)),
    ("PD", (2, 3)),
    ("MD", (0, 1)),
    ("PF", (0, 1)),
    ("MF", (2, 3)),
    ("PS", (0, 1)),
    ("MS", (2, 3)),
):
    NAMES += [(stem, j) for j in slices]
SEM = {name: i for i, name in enumerate(NAMES)}


def when(pred, fn):
    if pred is None:
        fn()
    else:
        pl.when(pred)(fn)


def kernel(
    cyc, off, vol, pri, dua, vn_out, dn_out,
    OWN, R1, R3, R2, X2, W, V, T, Z, FL, DU, FR, F1P, F1M, F2, FX, XF1, XF2,
    RP, RM, SP, SM, INM, INP, LS, PRI, VN, ss, rs, ls,
):
    tm = lax.axis_index("tm")
    s = lax.axis_index("space")
    h = tm // 32
    z = (tm // 4) % 8
    y = tm % 4
    pos = z // 2
    c = 4 * h + pos
    plus = (h * 32 + ((z + 2) % 8) * 4 + y, s)
    minus = (h * 32 + ((z + 6) % 8) * 4 + y, s)
    across = ((1 - h) * 32 + z * 4 + y, s)
    below = (tm, lax.max(s - 1, 0))
    above = (tm, lax.min(s + 1, 3))
    has_below = s > 0
    has_above = s < 3
    first, last = c == 0, c == 7
    is3, is4 = c == 3, c == 4
    inner = jnp.logical_and(c > 1, c < 6)
    outer = jnp.logical_not(inner)

    def copy(name, src, dst, target):
        i = SEM[name]
        return pltpu.make_async_remote_copy(
            src_ref=src, dst_ref=dst, send_sem=ss.at[i], recv_sem=rs.at[i],
            device_id=target, device_id_type=MESH,
        )

    sent = []

    def send(name, src, dst, target, pred=None):
        when(pred, lambda: copy(name, src, dst, target).start())
        sent.append((name, target, pred))

    def arrive(name, dst, pred=None):
        when(pred, lambda: copy(name, dst, dst, across).wait_recv())

    def img(ref, k):
        return ref.at[k, :, pl.ds(PAD, NY), :]

    class Split:
        def __init__(self, make):
            self.copies = [make(b, pl.ds(b * LANES, LANES)) for b in range(HALVES)]

        def start(self):
            for one in self.copies:
                one.start()

        def wait(self):
            for one in self.copies:
                one.wait()

    own_in = [
        Split(lambda b, cols, j=j: pltpu.make_async_copy(vol.at[0, j, :, cols], OWN.at[1 + j, b], ls.at[j, b]))
        for j in range(NZ)
    ]
    for j in (0, 3, 1, 2):
        own_in[j].start()

    barrier = pltpu.get_barrier_semaphore()
    for target, pred in ((plus, None), (minus, None), (across, None), (below, has_below), (above, has_above)):
        when(pred, lambda target=target: pl.semaphore_signal(barrier, inc=1, device_id=target, device_id_type=MESH))
    dual_in = Split(lambda b, cols: pltpu.make_async_copy(dua.at[0, :, :, :, cols], DU.at[:, :, b], ls.at[4, b]))
    prior_in = Split(lambda b, cols: pltpu.make_async_copy(pri.at[0, :, :, cols], PRI.at[:, b], ls.at[5, b]))
    pl.semaphore_wait(barrier, 3 + has_below.astype(jnp.int32) + has_above.astype(jnp.int32))

    not_p3 = pos < 3
    not_p0 = pos > 0
    not_first, not_last = jnp.logical_not(first), jnp.logical_not(last)

    def send_own(sign, j):
        src = OWN.at[1 + j]
        if sign > 0:
            name, target, inside, edge, spare, into = ("P", j), plus, not_p3, pos == 3, last, img(R3, 1 + j)
            direct = j >= 2
        else:
            name, target, inside, edge, spare, into = ("M", j), minus, not_p0, pos == 0, first, img(R1, 1 + j)
            direct = j < 2
        send(name, src, into, target, inside)
        if direct:
            arrive(("XV", j), V.at[j], spare)
            send(name, V.at[j], into, target, spare)
        else:
            send(name, src, W.at[j], target, edge)

    def send_across():
        for j in (3, 2):
            send(("XV", j), OWN.at[1 + j], V.at[j], across, c == 3)
        for j in (0, 1):
            send(("XV", j), OWN.at[1 + j], V.at[j], across, c == 4)

    def halo(i, ref, k, src=None, pred=None):
        own = ref is OWN
        at = (lambda k: ref.at[k]) if own else (lambda k: img(ref, k))
        both = lambda a: a if pred is None else jnp.logical_and(a, pred)
        if k == 1:
            send(("HL", i), at(1), at(5), below, both(has_below))
        else:
            send(("HH", i), at(4), at(0), above, both(has_above))

    def halo_arrive(i, ref, pred=None):
        own = ref is OWN
        at = (lambda k: ref.at[k]) if own else (lambda k: img(ref, k))
        both = lambda a: a if pred is None else jnp.logical_and(a, pred)
        arrive(("HL", i), at(5), both(has_above))
        arrive(("HH", i), at(0), both(has_below))

    own_in[0].wait()
    send_own(1, 0)
    own_in[3].wait()
    send_own(-1, 3)
    own_in[1].wait()
    send_own(1, 1)
    own_in[2].wait()
    send_own(-1, 2)
    send_across()
    halo(0, OWN, 1)
    halo(0, OWN, 4)
    dual_in.start()
    prior_in.start()

    zeros = jnp.zeros((6, HALVES, PAD, LANES), jnp.float32)
    for ref in (R1, R3, R2, X2):
        ref[:, :, pl.ds(0, PAD), :] = zeros
        ref[:, :, pl.ds(PAD + NY, PAD), :] = zeros
    for ref in (Z, FL):
        ref[:, pl.ds(0, PAD), :] = zeros[0]
        ref[:, pl.ds(PAD + NY, PAD), :] = zeros[0]

    @pl.when(s == 0)
    def _():
        T[0] = jnp.zeros((HALVES, NY, LANES), jnp.float32)

    @pl.when(s == 3)
    def _():
        T[5] = jnp.zeros((HALVES, NY, LANES), jnp.float32)

    def got_plus(j):
        if j < 2:
            arrive(("P", j), img(R3, 1 + j), not_p0)
            arrive(("P", j), W.at[j], pos == 0)
            send(("PR", j), img(R3, 1 + j), img(R2, 1 + j), plus, not_p0)
            send(("PR", j), W.at[j], img(R2, 1 + j), plus, pos == 0)
            send(("XW", j), W.at[j], img(R3, 1 + j), across, first)
            if j == 0:
                halo(2, R3, 1, pred=not_p0)
        else:
            arrive(("P", j), img(R3, 1 + j), not_first)
            if j == 3:
                halo(2, R3, 4, pred=not_first)

    def got_minus(j):
        if j >= 2:
            arrive(("M", j), img(R1, 1 + j), not_p3)
            arrive(("M", j), W.at[j], pos == 3)
            send(("MR", j), img(R1, 1 + j), img(R2, 1 + j), minus, not_p3)
            send(("MR", j), W.at[j], img(R2, 1 + j), minus, pos == 3)
            send(("XW", j), W.at[j], img(R1, 1 + j), across, last)
            if j == 3:
                halo(1, R1, 4, pred=not_p3)
        else:
            arrive(("M", j), img(R1, 1 + j), not_last)
            if j == 0:
                halo(1, R1, 1, pred=not_last)

    up = (0, 1, 3, 2)
    down = (3, 2, 0, 1)

    def own(rank):
        send_own(1, up[rank])
        send_own(-1, down[rank])

    def got(rank):
        got_plus(up[rank])
        got_minus(down[rank])

    def got_opposite(name, j):
        arrive((name, j), img(R2, 1 + j))
        send(("XO", j), img(R2, 1 + j), img(X2, 1 + j), across, outer)
        if j in (0, 3):
            halo(3, R2, 1 + j)

    lane = lax.broadcasted_iota(jnp.int32, (CHUNK, LANES), 1)
    left, right = lane == 0, lane == LANES - 1
    k_lo = 1 - has_below.astype(jnp.int32)
    k_hi = 5 + has_above.astype(jnp.int32)
    chunks = NY // CHUNK

    def pair(p, direction, ref, out, fresh_sum, order, emit):
        slot = jnp.int32(0)
        shift = jnp.int32(0)
        active = jnp.int32(0)
        for k in range(4):
            hit = cyc[0, k] == direction
            slot = slot + jnp.where(hit, k, 0)
            shift = shift + jnp.where(hit, off[0, k], 0)
            active = active + jnp.where(hit, 1, 0)
        live = active > 0

        def contrast(k, b, r):
            return ref[k, b, pl.ds(PAD - shift + r, CHUNK), :] - OWN[k, b, pl.ds(r, CHUNK), :]

        def squares(k, carry):
            for q in range(chunks):
                r = q * CHUNK
                x0, x1 = contrast(k, 0, r), contrast(k, 1, r)
                x0, x1 = x0 * x0, x1 * x1
                l0, l1 = pltpu.roll(x0, 1, 1), pltpu.roll(x1, 1, 1)
                r0, r1 = pltpu.roll(x0, LANES - 1, 1), pltpu.roll(x1, LANES - 1, 1)
                T[k, 0, pl.ds(r, CHUNK), :] = x0 + jnp.where(left, 0.0, l0) + jnp.where(right, r1, r0)
                T[k, 1, pl.ds(r, CHUNK), :] = x1 + jnp.where(left, l0, l1) + jnp.where(right, 0.0, r1)
            return carry

        lax.fori_loop(k_lo, k_hi, squares, 0)

        def update(j):
            for b in range(HALVES):
                for q in range(chunks):
                    rows = pl.ds(q * CHUNK, CHUNK)
                    Z[b, pl.ds(PAD + q * CHUNK, CHUNK), :] = T[j, b, rows, :] + T[j + 1, b, rows, :] + T[j + 2, b, rows, :]
                for q in range(chunks):
                    r = q * CHUNK
                    rows = pl.ds(r, CHUNK)
                    total = (
                        Z[b, pl.ds(PAD - 1 + r, CHUNK), :]
                        + Z[b, pl.ds(PAD + r, CHUNK), :]
                        + Z[b, pl.ds(PAD + 1 + r, CHUNK), :]
                    )
                    w = jnp.exp(total * (-1.0 / 108.0))
                    fresh = jnp.clip(DU[slot, j, b, rows, :] + 0.5 * w * contrast(j + 1, b, r), -0.3, 0.3)
                    fresh = jnp.where(live, fresh, 0.0)
                    FR[p, j, b, rows, :] = fresh
                    flux = w * fresh
                    if fresh_sum:
                        LS[j, b, rows, :] = flux
                    else:
                        LS[j, b, rows, :] = LS[j, b, rows, :] + flux
                    FL[b, pl.ds(PAD + r, CHUNK), :] = flux
                for q in range(chunks):
                    r = q * CHUNK
                    out[j, b, pl.ds(r, CHUNK), :] = FL[b, pl.ds(PAD + shift + r, CHUNK), :]

        for n, j in enumerate(order):
            update(j)
            if n > 0:
                emit(order[n - 1])
        emit(order[-1])

    forward = pos < 2
    def opposite(rank):
        got_opposite("PR", rank)
        got_opposite("MR", 3 - rank)

    def send_far(pred, j):
        if j < 2:
            send(("PF", j), F2.at[j], RP.at[j], plus, pred)
        else:
            send(("MF", j), F2.at[j], RM.at[j - 2], minus, pred)

    def pair_far():
        halo_arrive(3, R2)
        pair(2, jnp.where(forward, 2, -2), R2, F2, True, (0, 3, 1, 2), functools.partial(send_far, inner))

    def pair_across():
        for j in (0, 3, 1, 2):
            arrive(("XO", j), img(X2, 1 + j), inner)
            if j in (0, 3):
                halo(4, X2, 1 + j, pred=inner)
        halo_arrive(4, X2, inner)

        def emit(j):
            send(("FO", j), FX.at[j], XF2.at[j], across, inner)

        @pl.when(inner)
        def _():
            pair(3, jnp.where(forward, -2, 2), X2, FX, False, (0, 3, 1, 2), emit)

    def got_across():
        for j in (3, 2):
            arrive(("XW", j), img(R1, 1 + j), c == 3)
        halo(1, R1, 4, pred=c == 3)
        for j in (0, 1):
            arrive(("XW", j), img(R3, 1 + j), c == 4)
        halo(2, R3, 1, pred=c == 4)

    def pair_next():
        halo_arrive(1, R1, not_last)

        def emit(j):
            if j < 2:
                send(("FX", j), F1P.at[j], XF1.at[j], across, is3)
            else:
                send(("PD", j), F1P.at[j], INM.at[j], plus, not_last)

        @pl.when(not_last)
        def _():
            pair(0, 1, R1, F1P, False, (2, 3, 0, 1), emit)

    def pair_before():
        halo_arrive(2, R3, not_first)

        def emit(j):
            if j < 2:
                send(("MD", j), F1M.at[j], INP.at[j], minus, not_first)
            else:
                send(("FX", j), F1M.at[j], XF1.at[j], across, is4)

        @pl.when(not_first)
        def _():
            pair(1, -1, R3, F1M, False, (1, 0, 3, 2), emit)

    def far_outer():
        for j in (0, 3, 1, 2):
            arrive(("FO", j), XF2.at[j], outer)

            @pl.when(outer)
            def _():
                F2[j] = F2[j] + XF2[j]

            if j == 0 or j == 1:
                send(("PF", j), F2.at[j], RP.at[j], plus, outer)
            else:
                send(("MF", j), F2.at[j], RM.at[j - 2], minus, outer)

    halo_arrive(0, OWN)
    dual_in.wait()
    got(0)
    own(2)
    got(1)
    own(3)
    opposite(0)
    opposite(1)
    pair_far()
    got(2)
    pair_across()
    got(3)
    got_across()
    pair_next()
    pair_before()
    far_outer()

    for j in (0, 1):
        arrive(("FX", j), XF1.at[j], last)
    for j in (3, 2):
        arrive(("FX", j), XF1.at[j], first)

    def pass_on():
        for j in (2, 3):
            arrive(("PD", j), INM.at[j], first)
            send(("XD", j), INM.at[j], INM.at[j], across, first)
        for j in (1, 0):
            arrive(("MD", j), INP.at[j], last)
            send(("XD", j), INP.at[j], INP.at[j], across, last)

    def slot_out(k):
        cycle = cyc[0, k]
        hop = jnp.where(cycle > 0, 0, 1)
        far = jnp.where((cycle > 0) == forward, 2, 3)
        p = jnp.where(jnp.logical_or(cycle == 1, cycle == -1), hop, far)

        def put(j, carry):
            DU[k, j] = jnp.where(cycle != 0, FR[p, j], 0.0)
            return carry

        lax.fori_loop(0, NZ, put, 0)

    for k in range(4):
        slot_out(k)
    dual_out = Split(lambda b, cols: pltpu.make_async_copy(DU.at[:, :, b], dn_out.at[0, :, :, :, cols], ls.at[6, b]))
    dual_out.start()
    prior_in.wait()

    def start_volume(j, carry):
        VN[j] = OWN[1 + j] + 0.25 * LS[j] + 0.25 * PRI[j]
        return carry

    lax.fori_loop(0, NZ, start_volume, 0)

    def second(name, onward, rel, sums, base, spare, j, i, target, none, swap, dst):
        arrive((name, j), rel.at[i])

        @pl.when(none)
        def _():
            sums[i] = rel[i]

        @pl.when(swap)
        def _():
            sums[i] = rel[i] + spare[j]

        @pl.when(jnp.logical_not(jnp.logical_or(none, swap)))
        def _():
            sums[i] = rel[i] + base[j]

        send((onward, j), sums.at[i], dst.at[j], target)

    second("PF", "PS", RP, SP, F1P, XF1, 0, 0, plus, c == 3, last, INM)
    second("MF", "MS", RM, SM, F1M, XF1, 3, 1, minus, c == 4, first, INP)
    pass_on()
    second("PF", "PS", RP, SP, F1P, XF1, 1, 1, plus, c == 3, last, INM)
    second("MF", "MS", RM, SM, F1M, XF1, 2, 0, minus, c == 4, first, INP)

    def take(ref, j):
        VN[j] = VN[j] - 0.25 * ref[j]

    for j in (2, 3):
        arrive(("PD", j), INM.at[j], jnp.logical_and(c != 4, not_first))
        arrive(("XD", j), INM.at[j], c == 4)
        pl.when(not_first)(functools.partial(take, INM, j))
    for j in (1, 0):
        arrive(("MD", j), INP.at[j], jnp.logical_and(c != 3, not_last))
        arrive(("XD", j), INP.at[j], c == 3)
        pl.when(not_last)(functools.partial(take, INP, j))

    outs = []
    for name, ref, j in (("PS", INM, 0), ("MS", INP, 3), ("PS", INM, 1), ("MS", INP, 2)):
        arrive((name, j), ref.at[j])
        VN[j] = (VN[j] - 0.25 * ref[j]) / 1.25
        outs.append(
            Split(lambda b, cols, j=j: pltpu.make_async_copy(VN.at[j, b], vn_out.at[0, j, :, cols], ls.at[j, b]))
        )
        outs[-1].start()

    for name, target, pred in sent:
        when(pred, lambda: copy(name, OWN.at[0], OWN.at[0], target).wait_send())
    for out in outs:
        out.wait()
    dual_out.wait()


def shards(volume, prior_image, dual_pairs, pair_cycle, pair_offset):
    image = pltpu.VMEM((NZ + 2, HALVES, ROWS, LANES), jnp.float32)
    block = pltpu.VMEM((NZ, HALVES, NY, LANES), jnp.float32)
    half = pltpu.VMEM((2, HALVES, NY, LANES), jnp.float32)
    plane = pltpu.VMEM((HALVES, ROWS, LANES), jnp.float32)
    stack = pltpu.VMEM((NZ + 2, HALVES, NY, LANES), jnp.float32)
    slots = pltpu.VMEM((4, NZ, HALVES, NY, LANES), jnp.float32)
    smem = pl.BlockSpec(memory_space=pltpu.SMEM)
    anyspace = pl.BlockSpec(memory_space=pl.ANY)
    return pl.pallas_call(
        kernel,
        out_shape=(
            pltpu.VMEM(volume.shape, jnp.float32),
            pltpu.VMEM(dual_pairs.shape, jnp.float32),
        ),
        in_specs=[smem, smem, anyspace, anyspace, anyspace],
        out_specs=(anyspace, anyspace),
        scratch_shapes=[
            stack, image, image, image, image, block, block,
            stack, plane, plane, slots, slots,
            block, block, block, block, block, block,
            half, half, half, half, block, block,
            block, block, block,
            pltpu.SemaphoreType.DMA((len(NAMES),)),
            pltpu.SemaphoreType.DMA((len(NAMES),)),
            pltpu.SemaphoreType.DMA((7, HALVES)),
        ],
        compiler_params=pltpu.CompilerParams(collective_id=0, vmem_limit_bytes=61_790_000, has_side_effects=True),
    )(pair_cycle, pair_offset, volume, prior_image, dual_pairs)


def solution(mesh):
    return jax.shard_map(
        shards,
        mesh=mesh,
        in_specs=(
            P("tm", "space", None, None),
            P("tm", "space", None, None),
            P("tm", None, "space", None, None),
            P("tm", None),
            P("tm", None),
        ),
        out_specs=(P("tm", "space", None, None), P("tm", None, "space", None, None)),
        check_vma=False,
    )
```

profile of v0, /device:TPU:22, one launch (start us, length us, event | category | flops | bytes accessed | tf_op | source)
XLA Modules:
  0.0 158.3 jit_solution(10796256978954556887)
XLA Ops:
  0.6 154.6 %shard_map.68 = (f32[1,4,256,256]{3,2,1,0:T(8,128)S(1)}, f32[1,4,4,256,256]{4,3,2,1,0:T(8,128)S(1)}) custom-call(s32[1,4]{1,0:T(1,128)} %cyc.1, s32[1,4]{1,0:T(1,128)} %off.1, f32[1,4,256,256]{3,2,1,0:T(8,128)} %vol.1, f32[1,4,256,256]{3,2,1,0:T(8,128)} %pri.1, f32[1,4,4,256,256]{4,3,2,1,0:T(8,128)} %dua.1), custom_call_target="tpu_custom_call" | custom-call | tf_op jit(solution)/shard_map/pallas_call | solution.py:491
  155.3 1.0 copy.9
  156.2 2.0 %copy.10 = f32[1,4,4,256,256]{4,3,2,1,0:T(8,128)} copy(f32[1,4,4,256,256]{4,3,2,1,0:T(8,128)S(1)} %get-tuple-element.3) | data formatting | bytes 8388608
where the time goes:
time: 158 us
  Pallas kernels  155 us (98%)
  local copies, waits for them, and re-layouts  2.99 us (2%)
    pallas_call x1, Pallas kernels, shards(): pl.pallas_call(kernel, out_shape=(pltpu.VMEM(volume.shape, jnp.float32),...  155 us

commit v1 on v0

--- a/solution.py
+++ b/solution.py
@@ -47,11 +47,27 @@
         pl.when(pred)(fn)
 
 
+class Image:
+    def __init__(self, main, late=None, late_k=None):
+        self.main, self.late, self.late_k = main, late, late_k
+
+    def block(self, k):
+        if self.late is not None and k == self.late_k:
+            return self.late.at[:, pl.ds(PAD, NY), :]
+        return self.main.at[k, :, pl.ds(PAD, NY), :]
+
+    def load(self, k, b, start):
+        if self.late is not None and k == self.late_k:
+            return self.late[b, pl.ds(start, CHUNK), :]
+        return self.main[k, b, pl.ds(start, CHUNK), :]
+
+
 def kernel(
     cyc, off, vol, pri, dua, vn_out, dn_out,
-    OWN, R1, R3, R2, X2, W, V, T, Z, FL, DU, FR, F1P, F1M, F2, FX, XF1, XF2,
+    OWN, R1, R3, R2, X2, R1L, R3L, W, V, T, T1, T3, Z, FL, DU, FR, F1P, F1M, F2, FX, XF1, XF2,
     RP, RM, SP, SM, INM, INP, LS, PRI, VN, ss, rs, ls,
 ):
+    R1, R3, R2, X2 = Image(R1, R1L, 2), Image(R3, R3L, 3), Image(R2), Image(X2)
     tm = lax.axis_index("tm")
     s = lax.axis_index("space")
     h = tm // 32
@@ -88,7 +104,7 @@
         when(pred, lambda: copy(name, dst, dst, across).wait_recv())
 
     def img(ref, k):
-        return ref.at[k, :, pl.ds(PAD, NY), :]
+        return ref.block(k)
 
     class Split:
         def __init__(self, make):
@@ -172,20 +188,22 @@
     prior_in.start()
 
     zeros = jnp.zeros((6, HALVES, PAD, LANES), jnp.float32)
-    for ref in (R1, R3, R2, X2):
+    for ref in (R1.main, R3.main, R2.main, X2.main):
         ref[:, :, pl.ds(0, PAD), :] = zeros
         ref[:, :, pl.ds(PAD + NY, PAD), :] = zeros
-    for ref in (Z, FL):
+    for ref in (Z, FL, R1L, R3L):
         ref[:, pl.ds(0, PAD), :] = zeros[0]
         ref[:, pl.ds(PAD + NY, PAD), :] = zeros[0]
 
     @pl.when(s == 0)
     def _():
-        T[0] = jnp.zeros((HALVES, NY, LANES), jnp.float32)
+        for sums in (T, T1, T3):
+            sums[0] = jnp.zeros((HALVES, NY, LANES), jnp.float32)
 
     @pl.when(s == 3)
     def _():
-        T[5] = jnp.zeros((HALVES, NY, LANES), jnp.float32)
+        for sums in (T, T1, T3):
+            sums[5] = jnp.zeros((HALVES, NY, LANES), jnp.float32)
 
     def got_plus(j):
         if j < 2:
@@ -238,7 +256,7 @@
     k_hi = 5 + has_above.astype(jnp.int32)
     chunks = NY // CHUNK
 
-    def pair(p, direction, ref, out, fresh_sum, order, emit):
+    def pair(p, direction, ref, out, fresh_sum, T):
         slot = jnp.int32(0)
         shift = jnp.int32(0)
         active = jnp.int32(0)
@@ -250,9 +268,9 @@
         live = active > 0
 
         def contrast(k, b, r):
-            return ref[k, b, pl.ds(PAD - shift + r, CHUNK), :] - OWN[k, b, pl.ds(r, CHUNK), :]
-
-        def squares(k, carry):
+            return ref.load(k, b, PAD - shift + r) - OWN[k, b, pl.ds(r, CHUNK), :]
+
+        def squares(k):
             for q in range(chunks):
                 r = q * CHUNK
                 x0, x1 = contrast(k, 0, r), contrast(k, 1, r)
@@ -261,9 +279,6 @@
                 r0, r1 = pltpu.roll(x0, LANES - 1, 1), pltpu.roll(x1, LANES - 1, 1)
                 T[k, 0, pl.ds(r, CHUNK), :] = x0 + jnp.where(left, 0.0, l0) + jnp.where(right, r1, r0)
                 T[k, 1, pl.ds(r, CHUNK), :] = x1 + jnp.where(left, l0, l1) + jnp.where(right, 0.0, r1)
-            return carry
-
-        lax.fori_loop(k_lo, k_hi, squares, 0)
 
         def update(j):
             for b in range(HALVES):
@@ -292,6 +307,16 @@
                     r = q * CHUNK
                     out[j, b, pl.ds(r, CHUNK), :] = FL[b, pl.ds(PAD + shift + r, CHUNK), :]
 
+        return squares, update
+
+    def all_squares(squares):
+        def one(k, carry):
+            squares(k)
+            return carry
+
+        lax.fori_loop(k_lo, k_hi, one, 0)
+
+    def updates(update, order, emit):
         for n, j in enumerate(order):
             update(j)
             if n > 0:
@@ -311,7 +336,9 @@
 
     def pair_far():
         halo_arrive(3, R2)
-        pair(2, jnp.where(forward, 2, -2), R2, F2, True, (0, 3, 1, 2), functools.partial(send_far, inner))
+        squares, update = pair(2, jnp.where(forward, 2, -2), R2, F2, True, T)
+        all_squares(squares)
+        updates(update, (0, 3, 1, 2), functools.partial(send_far, inner))
 
     def pair_across():
         for j in (0, 3, 1, 2):
@@ -325,7 +352,9 @@
 
         @pl.when(inner)
         def _():
-            pair(3, jnp.where(forward, -2, 2), X2, FX, False, (0, 3, 1, 2), emit)
+            squares, update = pair(3, jnp.where(forward, -2, 2), X2, FX, False, T)
+            all_squares(squares)
+            updates(update, (0, 3, 1, 2), emit)
 
     def got_across():
         for j in (3, 2):
@@ -335,31 +364,74 @@
             arrive(("XW", j), img(R3, 1 + j), c == 4)
         halo(2, R3, 1, pred=c == 4)
 
-    def pair_next():
+    next_squares, next_update = pair(0, 1, R1, F1P, False, T1)
+    before_squares, before_update = pair(1, -1, R3, F1M, False, T3)
+
+    def next_emit(j):
+        if j < 2:
+            send(("FX", j), F1P.at[j], XF1.at[j], across, is3)
+        else:
+            send(("PD", j), F1P.at[j], INM.at[j], plus, not_last)
+
+    def before_emit(j):
+        if j < 2:
+            send(("MD", j), F1M.at[j], INP.at[j], minus, not_first)
+        else:
+            send(("FX", j), F1M.at[j], XF1.at[j], across, is4)
+
+    def early():
         halo_arrive(1, R1, not_last)
 
-        def emit(j):
-            if j < 2:
-                send(("FX", j), F1P.at[j], XF1.at[j], across, is3)
-            else:
-                send(("PD", j), F1P.at[j], INM.at[j], plus, not_last)
-
         @pl.when(not_last)
         def _():
-            pair(0, 1, R1, F1P, False, (2, 3, 0, 1), emit)
-
-    def pair_before():
+            pl.when(has_above)(functools.partial(next_squares, 5))
+            next_squares(4)
+            next_squares(3)
+            next_update(3)
+
         halo_arrive(2, R3, not_first)
 
-        def emit(j):
-            if j < 2:
-                send(("MD", j), F1M.at[j], INP.at[j], minus, not_first)
-            else:
-                send(("FX", j), F1M.at[j], XF1.at[j], across, is4)
-
         @pl.when(not_first)
         def _():
-            pair(1, -1, R3, F1M, False, (1, 0, 3, 2), emit)
+            pl.when(has_below)(functools.partial(before_squares, 0))
+            before_squares(1)
+            before_squares(2)
+            before_update(0)
+
+        next_emit(3)
+        before_emit(0)
+
+        @pl.when(not_last)
+        def _():
+            pl.when(has_below)(functools.partial(next_squares, 0))
+            next_squares(1)
+
+        @pl.when(not_first)
+        def _():
+            pl.when(has_above)(functools.partial(before_squares, 5))
+            before_squares(4)
+
+    def late():
+        @pl.when(not_last)
+        def _():
+            next_squares(2)
+            next_update(2)
+
+        @pl.when(not_first)
+        def _():
+            before_squares(3)
+            before_update(1)
+
+        next_emit(2)
+        before_emit(1)
+
+        @pl.when(not_last)
+        def _():
+            updates(next_update, (0, 1), next_emit)
+
+        @pl.when(not_first)
+        def _():
+            updates(before_update, (3, 2), before_emit)
 
     def far_outer():
         for j in (0, 3, 1, 2):
@@ -385,10 +457,10 @@
     pair_far()
     got(2)
     pair_across()
+    got_across()
+    early()
     got(3)
-    got_across()
-    pair_next()
-    pair_before()
+    late()
     far_outer()
 
     for j in (0, 1):
@@ -397,10 +469,10 @@
         arrive(("FX", j), XF1.at[j], first)
 
     def pass_on():
-        for j in (2, 3):
+        for j in (3, 2):
             arrive(("PD", j), INM.at[j], first)
             send(("XD", j), INM.at[j], INM.at[j], across, first)
-        for j in (1, 0):
+        for j in (0, 1):
             arrive(("MD", j), INP.at[j], last)
             send(("XD", j), INP.at[j], INP.at[j], across, last)
 
@@ -497,8 +569,8 @@
         in_specs=[smem, smem, anyspace, anyspace, anyspace],
         out_specs=(anyspace, anyspace),
         scratch_shapes=[
-            stack, image, image, image, image, block, block,
-            stack, plane, plane, slots, slots,
+            stack, image, image, image, image, plane, plane, block, block,
+            stack, stack, stack, plane, plane, slots, slots,
             block, block, block, block, block, block,
             half, half, half, half, block, block,
             block, block, block,

time: 158 us -> 155 us (0.981)
  Pallas kernels: 155 us -> 151 us
    pallas_call x1, Pallas kernels: 155 us -> 151 us  [shards(): pl.pallas_call(kernel, out_shape=(pltpu.VMEM(volume.shape, jnp.float32),...]
where the time goes in v1:
time: 155 us
  Pallas kernels  151 us (97%)
  local copies, waits for them, and re-layouts  2.99 us (2%)
    pallas_call x1, Pallas kernels, shards(): pl.pallas_call(kernel, out_shape=(pltpu.VMEM(volume.shape, jnp.float32),...  151 us

profile of v1, /device:TPU:22, one launch (start us, length us, event | category | flops | bytes accessed | tf_op | source)
XLA Modules:
  0.0 154.8 jit_solution(15260978840170500873)
XLA Ops:
  0.6 151.2 %shard_map.68 = (f32[1,4,256,256]{3,2,1,0:T(8,128)S(1)}, f32[1,4,4,256,256]{4,3,2,1,0:T(8,128)S(1)}) custom-call(s32[1,4]{1,0:T(1,128)} %cyc.1, s32[1,4]{1,0:T(1,128)} %off.1, f32[1,4,256,256]{3,2,1,0:T(8,128)} %vol.1, f32[1,4,256,256]{3,2,1,0:T(8,128)} %pri.1, f32[1,4,4,256,256]{4,3,2,1,0:T(8,128)} %dua.1), custom_call_target="tpu_custom_call" | custom-call | tf_op jit(solution)/shard_map/pallas_call | solution.py:563
  151.8 1.0 copy.9
  152.8 2.0 %copy.10 = f32[1,4,4,256,256]{4,3,2,1,0:T(8,128)} copy(f32[1,4,4,256,256]{4,3,2,1,0:T(8,128)S(1)} %get-tuple-element.3) | data formatting | bytes 8388608

commit v2 on v1

--- a/solution.py
+++ b/solution.py
@@ -535,20 +535,29 @@
         arrive(("XD", j), INP.at[j], c == 3)
         pl.when(not_last)(functools.partial(take, INP, j))
 
-    outs = []
     for name, ref, j in (("PS", INM, 0), ("MS", INP, 3), ("PS", INM, 1), ("MS", INP, 2)):
         arrive((name, j), ref.at[j])
-        VN[j] = (VN[j] - 0.25 * ref[j]) / 1.25
-        outs.append(
-            Split(lambda b, cols, j=j: pltpu.make_async_copy(VN.at[j, b], vn_out.at[0, j, :, cols], ls.at[j, b]))
-        )
-        outs[-1].start()
+        for b in range(HALVES):
+            vn_out[0, j, :, pl.ds(b * LANES, LANES)] = (VN[j, b] - 0.25 * ref[j, b]) / 1.25
 
     for name, target, pred in sent:
         when(pred, lambda: copy(name, OWN.at[0], OWN.at[0], target).wait_send())
-    for out in outs:
-        out.wait()
     dual_out.wait()
+
+
+def results(volume_in, dual_in, volume_out, dual_out, sems):
+    copies = []
+    for k in range(4):
+        for half in range(2):
+            rows = pl.ds(2 * half, 2)
+            copies.append(pltpu.make_async_copy(dual_in.at[0, k, rows], dual_out.at[0, k, rows], sems.at[k, half]))
+    for half in range(2):
+        rows = pl.ds(2 * half, 2)
+        copies.append(pltpu.make_async_copy(volume_in.at[0, rows], volume_out.at[0, rows], sems.at[4, half]))
+    for one in copies:
+        one.start()
+    for one in copies:
+        one.wait()
 
 
 def shards(volume, prior_image, dual_pairs, pair_cycle, pair_offset):
@@ -560,14 +569,14 @@
     slots = pltpu.VMEM((4, NZ, HALVES, NY, LANES), jnp.float32)
     smem = pl.BlockSpec(memory_space=pltpu.SMEM)
     anyspace = pl.BlockSpec(memory_space=pl.ANY)
-    return pl.pallas_call(
+    volume_next, dual_next = pl.pallas_call(
         kernel,
         out_shape=(
             pltpu.VMEM(volume.shape, jnp.float32),
             pltpu.VMEM(dual_pairs.shape, jnp.float32),
         ),
         in_specs=[smem, smem, anyspace, anyspace, anyspace],
-        out_specs=(anyspace, anyspace),
+        out_specs=(pl.BlockSpec(memory_space=pltpu.VMEM), anyspace),
         scratch_shapes=[
             stack, image, image, image, image, plane, plane, block, block,
             stack, stack, stack, plane, plane, slots, slots,
@@ -580,6 +589,17 @@
         ],
         compiler_params=pltpu.CompilerParams(collective_id=0, vmem_limit_bytes=61_790_000, has_side_effects=True),
     )(pair_cycle, pair_offset, volume, prior_image, dual_pairs)
+    return pl.pallas_call(
+        results,
+        out_shape=(
+            jax.ShapeDtypeStruct(volume.shape, jnp.float32),
+            jax.ShapeDtypeStruct(dual_pairs.shape, jnp.float32),
+        ),
+        in_specs=[anyspace, anyspace],
+        out_specs=(anyspace, anyspace),
+        scratch_shapes=[pltpu.SemaphoreType.DMA((5, 2))],
+        compiler_params=pltpu.CompilerParams(vmem_limit_bytes=1024 * 1024),
+    )(volume_next, dual_next)
 
 
 def solution(mesh):

time: 155 us -> 155 us (level)
  Pallas kernels: 151 us -> 154 us
  local copies, waits for them, and re-layouts: 2.99 us -> 0 us
    unnamed x2 -> x0, local copies, waits for them, and re-layouts: 2.99 us -> none
    pallas_call x0 -> x1, Pallas kernels: none -> 2.42 us  [shards(): pl.pallas_call(results, out_shape=(jax.ShapeDtypeStruct(volume.shape, jnp...]
where the time goes in v2:
time: 155 us; the launch traced here: 154 us
  Pallas kernels  154 us (99%)
    pallas_call x1, Pallas kernels, shards(): pl.pallas_call(kernel, out_shape=(pltpu.VMEM(volume.shape, jnp.float32),...  151 us

profile of v2, /device:TPU:22, one launch (start us, length us, event | category | flops | bytes accessed | tf_op | source)
XLA Modules:
  0.0 154.2 jit_solution(15528817990963121167)
XLA Ops:
  0.6 151.1 %shard_map.68 = (f32[1,4,256,256]{3,2,1,0:T(8,128)S(1)}, f32[1,4,4,256,256]{4,3,2,1,0:T(8,128)S(1)}) custom-call(s32[1,4]{1,0:T(1,128)} %cyc.1, s32[1,4]{1,0:T(1,128)} %off.1, f32[1,4,256,256]{3,2,1,0:T(8,128)} %vol.1, f32[1,4,256,256]{3,2,1,0:T(8,128)} %pri.1, f32[1,4,4,256,256]{4,3,2,1,0:T(8,128)} %dua.1), custom_call_target="tpu_custom_call" | custom-call | tf_op jit(solution)/shard_map/pallas_call | solution.py:572
  151.7 2.4 %shard_map.69 = (f32[1,4,256,256]{3,2,1,0:T(8,128)}, f32[1,4,4,256,256]{4,3,2,1,0:T(8,128)}) custom-call(f32[1,4,256,256]{3,2,1,0:T(8,128)S(1)} %get-tuple-element.4.volume_in, f32[1,4,4,256,256]{4,3,2,1,0:T(8,128)S(1)} %get-tuple-element.5.dual_in), custom_call_target="tpu_custom_call" | custom-call | tf_op jit(solution)/shard_map/pallas_call | solution.py:592

commit v3 on v2

--- a/solution.py
+++ b/solution.py
@@ -547,13 +547,10 @@
 
 def results(volume_in, dual_in, volume_out, dual_out, sems):
     copies = []
-    for k in range(4):
-        for half in range(2):
-            rows = pl.ds(2 * half, 2)
-            copies.append(pltpu.make_async_copy(dual_in.at[0, k, rows], dual_out.at[0, k, rows], sems.at[k, half]))
-    for half in range(2):
-        rows = pl.ds(2 * half, 2)
-        copies.append(pltpu.make_async_copy(volume_in.at[0, rows], volume_out.at[0, rows], sems.at[4, half]))
+    for j in range(NZ):
+        for k in range(4):
+            copies.append(pltpu.make_async_copy(dual_in.at[0, k, j], dual_out.at[0, k, j], sems.at[k, j]))
+        copies.append(pltpu.make_async_copy(volume_in.at[0, j], volume_out.at[0, j], sems.at[4, j]))
     for one in copies:
         one.start()
     for one in copies:
@@ -597,7 +594,7 @@
         ),
         in_specs=[anyspace, anyspace],
         out_specs=(anyspace, anyspace),
-        scratch_shapes=[pltpu.SemaphoreType.DMA((5, 2))],
+        scratch_shapes=[pltpu.SemaphoreType.DMA((5, NZ))],
         compiler_params=pltpu.CompilerParams(vmem_limit_bytes=1024 * 1024),
     )(volume_next, dual_next)
 

time: 155 us -> 155 us (level)
  no operation moved by 1% of the time
where the time goes in v3:
time: 155 us; the launch traced here: 154 us
  Pallas kernels  154 us (99%)
    pallas_call x1, Pallas kernels, shards(): pl.pallas_call(kernel, out_shape=(pltpu.VMEM(volume.shape, jnp.float32),...  151 us

profile of v3, /device:TPU:22, one launch (start us, length us, event | category | flops | bytes accessed | tf_op | source)
XLA Modules:
  0.0 154.3 jit_solution(4243291910442744954)
XLA Ops:
  0.6 151.2 %shard_map.68 = (f32[1,4,256,256]{3,2,1,0:T(8,128)S(1)}, f32[1,4,4,256,256]{4,3,2,1,0:T(8,128)S(1)}) custom-call(s32[1,4]{1,0:T(1,128)} %cyc.1, s32[1,4]{1,0:T(1,128)} %off.1, f32[1,4,256,256]{3,2,1,0:T(8,128)} %vol.1, f32[1,4,256,256]{3,2,1,0:T(8,128)} %pri.1, f32[1,4,4,256,256]{4,3,2,1,0:T(8,128)} %dua.1), custom_call_target="tpu_custom_call" | custom-call | tf_op jit(solution)/shard_map/pallas_call | solution.py:569
  151.8 2.5 %shard_map.69 = (f32[1,4,256,256]{3,2,1,0:T(8,128)}, f32[1,4,4,256,256]{4,3,2,1,0:T(8,128)}) custom-call(f32[1,4,256,256]{3,2,1,0:T(8,128)S(1)} %get-tuple-element.4.volume_in, f32[1,4,4,256,256]{4,3,2,1,0:T(8,128)S(1)} %get-tuple-element.5.dual_in), custom_call_target="tpu_custom_call" | custom-call | tf_op jit(solution)/shard_map/pallas_call | solution.py:589
